TPU v7x, 32 devices: a whole 2x2x4 slice. The times are simulated.
32 devices in a mesh: fac: 8 (over z, y), cust: 4 (over x, core).
Axes of the slice: x: 2, y: 2, z: 4, core: 2. Of those that a mesh axis runs over, the one named last changes fastest.
Arguments:
- fac_coords: bfloat16 [4096, 128], P('fac'), may hold values from -6 to 6
- cust_coords: bfloat16 [65536, 128], P(('cust', 'fac')), may hold values from -6 to 6
- open_flags: int32 [4096], P('fac'), may hold values 0 or 1
- demand: int32 [65536], P('cust'), may hold values from 1 to 4
- fixed_cost: float32 [4096], P('fac'), may hold values from 0 to 64
- capacity: float32 [4096], P('fac'), may hold values from 32 to 128
- cap_mult: float32 [4096], P('fac'), may hold values from 0 to 0.1
- cover_mult: float32 [65536], P('cust'), may hold values from 0 to 2, as said below
Outputs:
- cover_final: float32 [65536], P('cust')
- cap_final: float32 [4096], P('fac')
- bounds: float32 [3], replicated
Inputs may be any that keep to these rules, and one draw needn't show every extreme that they name: `cover_mult`: initial coverage multipliers, all in one band of width 0.4.
All inputs are finite; a program needn't handle non-finite values. No bound on the sum of `open_flags` on one device may be relied on, other than what follows from the above.
Results may differ from a plain program's by a relative error of at most 0.0003.
Values may be sent and summed in bfloat16 or wider, within the bound.
A program may use at most 64 MiB of HBM per device.

v0:
```python
import math

import jax
import jax.numpy as jnp
from jax import lax
from jax.sharding import PartitionSpec as P

ITERS = 3


def grouped_sum(values):
    length = values.shape[-1]
    parts = values.reshape(values.shape[:-1] + (length // 128, 128))
    return jnp.sum(jnp.sum(parts, axis=-1), axis=-1)


def local(fac_coords, cust_coords, open_flags, demand, fixed_cost, capacity, cap_mult, cover_mult):
    tau = 0.1
    coords_all = lax.all_gather(cust_coords, "fac", axis=0, tiled=True)
    n_cols = coords_all.shape[0]
    width = coords_all.shape[1]
    n_rows = fac_coords.shape[0]
    total_cust = n_cols * lax.axis_size("cust")
    block = math.gcd(n_cols, 2048)
    n_blocks = n_cols // block
    opened = open_flags.astype(jnp.float32)
    weight = demand.astype(jnp.float32)
    pnorm = jnp.sum(fac_coords.astype(jnp.float32) ** 2, axis=1)
    qnorm = jnp.sum(coords_all.astype(jnp.float32) ** 2, axis=1)
    coord_blocks = coords_all.reshape(n_blocks, block, width)
    qnorm_blocks = qnorm.reshape(n_blocks, block)
    weight_blocks = weight.reshape(n_blocks, block)
    lam = cover_mult
    mu = cap_mult
    bound_list = []
    for step in range(ITERS):
        size = 0.1 / (step + 1)
        lam_blocks = lam.reshape(n_blocks, block)

        def one_block(carry, pieces):
            load_acc, soft_acc = carry
            cols, qn, lam_b, wt_b = pieces
            dots = lax.dot_general(
                fac_coords, cols, (((1,), (1,)), ((), ())), preferred_element_type=jnp.float32
            )
            cost = (pnorm[:, None] + qn[None, :] - 2.0 * dots) / width
            zval = (lam_b[None, :] - cost - mu[:, None] * wt_b[None, :]) / tau
            share = opened[:, None] * jax.nn.sigmoid(zval)
            load_acc = load_acc + grouped_sum(share * wt_b[None, :])
            soft_acc = soft_acc + grouped_sum(jax.nn.softplus(zval) * wt_b[None, :])
            return ((load_acc, soft_acc), jnp.sum(share, axis=0))

        zeros_rows = jnp.zeros((n_rows,), jnp.float32)
        carry, cover_parts = lax.scan(
            one_block,
            (zeros_rows, zeros_rows),
            (coord_blocks, qnorm_blocks, lam_blocks, weight_blocks),
        )
        cover_part = cover_parts.reshape(n_cols)
        soft_part = -tau * opened * carry[1]
        lam_local = grouped_sum(weight * lam)
        facility_local = opened * fixed_cost - mu * capacity
        load, soft, lam_total = lax.psum((carry[0], soft_part, lam_local), "cust")
        row_total = grouped_sum(facility_local + soft)
        cover, row_sum = lax.psum((cover_part, row_total), "fac")
        new_lam = lam + size * weight * (1.0 - cover) / (1.0 + cover)
        bound = (row_sum + lam_total) / total_cust
        bound_list.append(bound)
        lam = new_lam
        mu = jnp.maximum(0.0, mu + size * (load - capacity) / (load + capacity))
    return (lam, mu, jnp.stack(bound_list))


def solution(mesh):
    return jax.shard_map(
        local,
        mesh=mesh,
        in_specs=(
            P("fac", None),
            P(("cust", "fac"), None),
            P("fac"),
            P("cust"),
            P("fac"),
            P("fac"),
            P("fac"),
            P("cust"),
        ),
        out_specs=(P("cust"), P("fac"), P()),
        check_vma=False,
    )
```

profile of v0, /device:TPU:0, one launch (start us, length us, event | category | flops | bytes accessed | tf_op | source)
XLA Modules:
  0.0 473.9 jit_solution(15274419989091801093)
XLA Ops:
  11.5 74.2 %all-gather.2.cloned.1.call-done = bf16[16384,128]{1,0:T(8,128)(2,1)} async-done(((bf16[2048,128]{1,0:T(8,128)(2,1)}), bf16[16384,128]{1,0:T(8,128)(2,1)}) %all-gather.2.cloned.1.call-update) | async-done | bytes 4194320 | tf_op jit(solution)/shard_map/all_gather | solution.py:19
  89.7 55.0 %while.45 = (s32[]{:T(128)}, f32[512]{0:T(512)S(1)}, f32[512]{0:T(512)S(1)}, f32[8,2048]{1,0:T(8,128)S(1)}, f32[512]{0:T(512)S(1)}, /*index=5*/f32[8,2048]{1,0:T...) while((s32[]{:T(128)}, f32[512]{0:T(512)S(1)}, ...), condition=%wide.region_6.7_spmd.clone, body=%wide.region_2.6_spmd.clone.sunk | while | flops 292551680 | bytes 776363 | solution.py:54
  89.8 6.6 %fusion.40 = (f32[512]{0:T(512)S(1)}, f32[512]{0:T(512)S(1)}, f32[2048]{0:T(1024)S(1)}) fusion(f32[2048]{0:T(1024)S(1)} %bitcast.116, f32[512]{0:T(512)S(1)} %get-tuple-element.710, f32[512]{0:T(512)S(1)} %get-tuple-element.716, bf16[512,128]{1,0:T(8,128)(2,1)S(1)} %get-tuple-element.715, bf16[8,2048,128]{2,1,0:T(8,128)(2,1)} %get-tuple-element.714, ...), kind=kOutput, calls=%fused_computation.2.clone.1 | convolution fusion | flops 292549632 | bytes 698372 | tf_op jit(solution)/shard_map/while/body/eval_jaxpr/dot_general | solution.py:43
  96.7 6.6 %fusion.40 = (f32[512]{0:T(512)S(1)}, f32[512]{0:T(512)S(1)}, f32[2048]{0:T(1024)S(1)}) fusion(f32[2048]{0:T(1024)S(1)} %bitcast.116, f32[512]{0:T(512)S(1)} %get-tuple-element.710, f32[512]{0:T(512)S(1)} %get-tuple-element.716, bf16[512,128]{1,0:T(8,128)(2,1)S(1)} %get-tuple-element.715, bf16[8,2048,128]{2,1,0:T(8,128)(2,1)} %get-tuple-element.714, ...), kind=kOutput, calls=%fused_computation.2.clone.1 | convolution fusion | flops 292549632 | bytes 698372 | tf_op jit(solution)/shard_map/while/body/eval_jaxpr/dot_general | solution.py:43
  103.5 6.6 %fusion.40 = (f32[512]{0:T(512)S(1)}, f32[512]{0:T(512)S(1)}, f32[2048]{0:T(1024)S(1)}) fusion(f32[2048]{0:T(1024)S(1)} %bitcast.116, f32[512]{0:T(512)S(1)} %get-tuple-element.710, f32[512]{0:T(512)S(1)} %get-tuple-element.716, bf16[512,128]{1,0:T(8,128)(2,1)S(1)} %get-tuple-element.715, bf16[8,2048,128]{2,1,0:T(8,128)(2,1)} %get-tuple-element.714, ...), kind=kOutput, calls=%fused_computation.2.clone.1 | convolution fusion | flops 292549632 | bytes 698372 | tf_op jit(solution)/shard_map/while/body/eval_jaxpr/dot_general | solution.py:43
  110.4 6.6 %fusion.40 = (f32[512]{0:T(512)S(1)}, f32[512]{0:T(512)S(1)}, f32[2048]{0:T(1024)S(1)}) fusion(f32[2048]{0:T(1024)S(1)} %bitcast.116, f32[512]{0:T(512)S(1)} %get-tuple-element.710, f32[512]{0:T(512)S(1)} %get-tuple-element.716, bf16[512,128]{1,0:T(8,128)(2,1)S(1)} %get-tuple-element.715, bf16[8,2048,128]{2,1,0:T(8,128)(2,1)} %get-tuple-element.714, ...), kind=kOutput, calls=%fused_computation.2.clone.1 | convolution fusion | flops 292549632 | bytes 698372 | tf_op jit(solution)/shard_map/while/body/eval_jaxpr/dot_general | solution.py:43
  117.3 6.6 %fusion.40 = (f32[512]{0:T(512)S(1)}, f32[512]{0:T(512)S(1)}, f32[2048]{0:T(1024)S(1)}) fusion(f32[2048]{0:T(1024)S(1)} %bitcast.116, f32[512]{0:T(512)S(1)} %get-tuple-element.710, f32[512]{0:T(512)S(1)} %get-tuple-element.716, bf16[512,128]{1,0:T(8,128)(2,1)S(1)} %get-tuple-element.715, bf16[8,2048,128]{2,1,0:T(8,128)(2,1)} %get-tuple-element.714, ...), kind=kOutput, calls=%fused_computation.2.clone.1 | convolution fusion | flops 292549632 | bytes 698372 | tf_op jit(solution)/shard_map/while/body/eval_jaxpr/dot_general | solution.py:43
  124.2 6.6 %fusion.40 = (f32[512]{0:T(512)S(1)}, f32[512]{0:T(512)S(1)}, f32[2048]{0:T(1024)S(1)}) fusion(f32[2048]{0:T(1024)S(1)} %bitcast.116, f32[512]{0:T(512)S(1)} %get-tuple-element.710, f32[512]{0:T(512)S(1)} %get-tuple-element.716, bf16[512,128]{1,0:T(8,128)(2,1)S(1)} %get-tuple-element.715, bf16[8,2048,128]{2,1,0:T(8,128)(2,1)} %get-tuple-element.714, ...), kind=kOutput, calls=%fused_computation.2.clone.1 | convolution fusion | flops 292549632 | bytes 698372 | tf_op jit(solution)/shard_map/while/body/eval_jaxpr/dot_general | solution.py:43
  131.1 6.6 %fusion.40 = (f32[512]{0:T(512)S(1)}, f32[512]{0:T(512)S(1)}, f32[2048]{0:T(1024)S(1)}) fusion(f32[2048]{0:T(1024)S(1)} %bitcast.116, f32[512]{0:T(512)S(1)} %get-tuple-element.710, f32[512]{0:T(512)S(1)} %get-tuple-element.716, bf16[512,128]{1,0:T(8,128)(2,1)S(1)} %get-tuple-element.715, bf16[8,2048,128]{2,1,0:T(8,128)(2,1)} %get-tuple-element.714, ...), kind=kOutput, calls=%fused_computation.2.clone.1 | convolution fusion | flops 292549632 | bytes 698372 | tf_op jit(solution)/shard_map/while/body/eval_jaxpr/dot_general | solution.py:43
  137.9 6.6 %fusion.40 = (f32[512]{0:T(512)S(1)}, f32[512]{0:T(512)S(1)}, f32[2048]{0:T(1024)S(1)}) fusion(f32[2048]{0:T(1024)S(1)} %bitcast.116, f32[512]{0:T(512)S(1)} %get-tuple-element.710, f32[512]{0:T(512)S(1)} %get-tuple-element.716, bf16[512,128]{1,0:T(8,128)(2,1)S(1)} %get-tuple-element.715, bf16[8,2048,128]{2,1,0:T(8,128)(2,1)} %get-tuple-element.714, ...), kind=kOutput, calls=%fused_computation.2.clone.1 | convolution fusion | flops 292549632 | bytes 698372 | tf_op jit(solution)/shard_map/while/body/eval_jaxpr/dot_general | solution.py:43
  151.1 62.2 %all-reduce.6.cloned.1.call-done = f32[16384]{0:T(1024)} async-done(((f32[16384]{0:T(1024)}), f32[16384]{0:T(1024)}) %all-reduce.6.cloned.1.call-update) | async-done | bytes 65552 | tf_op jit(solution)/shard_map/psum | solution.py:65
  214.3 55.0 %while.46 = (s32[]{:T(128)}, f32[512]{0:T(512)S(1)}, f32[512]{0:T(512)S(1)}, f32[8,2048]{1,0:T(8,128)S(1)}, f32[512]{0:T(512)S(1)}, /*index=5*/f32[8,2048]{1,0:T...) while((s32[]{:T(128)}, f32[512]{0:T(512)S(1)}, ...), condition=%wide.region_13.14_spmd.clone, body=%wide.region_9.13_spmd.clone.sunk | while | flops 292551680 | bytes 776363 | solution.py:54
  214.4 6.6 %fusion.42 = (f32[512]{0:T(512)S(1)}, f32[512]{0:T(512)S(1)}, f32[2048]{0:T(1024)S(1)}) fusion(f32[2048]{0:T(1024)S(1)} %bitcast.119, f32[512]{0:T(512)S(1)} %get-tuple-element.752, f32[512]{0:T(512)S(1)} %get-tuple-element.758, bf16[512,128]{1,0:T(8,128)(2,1)S(1)} %get-tuple-element.757, bf16[8,2048,128]{2,1,0:T(8,128)(2,1)} %get-tuple-element.756, ...), kind=kOutput, calls=%fused_computation.21.clone.1 | convolution fusion | flops 292549632 | bytes 698372 | tf_op jit(solution)/shard_map/while/body/eval_jaxpr/dot_general | solution.py:43
  221.2 6.6 %fusion.42 = (f32[512]{0:T(512)S(1)}, f32[512]{0:T(512)S(1)}, f32[2048]{0:T(1024)S(1)}) fusion(f32[2048]{0:T(1024)S(1)} %bitcast.119, f32[512]{0:T(512)S(1)} %get-tuple-element.752, f32[512]{0:T(512)S(1)} %get-tuple-element.758, bf16[512,128]{1,0:T(8,128)(2,1)S(1)} %get-tuple-element.757, bf16[8,2048,128]{2,1,0:T(8,128)(2,1)} %get-tuple-element.756, ...), kind=kOutput, calls=%fused_computation.21.clone.1 | convolution fusion | flops 292549632 | bytes 698372 | tf_op jit(solution)/shard_map/while/body/eval_jaxpr/dot_general | solution.py:43
  228.1 6.6 %fusion.42 = (f32[512]{0:T(512)S(1)}, f32[512]{0:T(512)S(1)}, f32[2048]{0:T(1024)S(1)}) fusion(f32[2048]{0:T(1024)S(1)} %bitcast.119, f32[512]{0:T(512)S(1)} %get-tuple-element.752, f32[512]{0:T(512)S(1)} %get-tuple-element.758, bf16[512,128]{1,0:T(8,128)(2,1)S(1)} %get-tuple-element.757, bf16[8,2048,128]{2,1,0:T(8,128)(2,1)} %get-tuple-element.756, ...), kind=kOutput, calls=%fused_computation.21.clone.1 | convolution fusion | flops 292549632 | bytes 698372 | tf_op jit(solution)/shard_map/while/body/eval_jaxpr/dot_general | solution.py:43
  235.0 6.6 %fusion.42 = (f32[512]{0:T(512)S(1)}, f32[512]{0:T(512)S(1)}, f32[2048]{0:T(1024)S(1)}) fusion(f32[2048]{0:T(1024)S(1)} %bitcast.119, f32[512]{0:T(512)S(1)} %get-tuple-element.752, f32[512]{0:T(512)S(1)} %get-tuple-element.758, bf16[512,128]{1,0:T(8,128)(2,1)S(1)} %get-tuple-element.757, bf16[8,2048,128]{2,1,0:T(8,128)(2,1)} %get-tuple-element.756, ...), kind=kOutput, calls=%fused_computation.21.clone.1 | convolution fusion | flops 292549632 | bytes 698372 | tf_op jit(solution)/shard_map/while/body/eval_jaxpr/dot_general | solution.py:43
  241.8 6.6 %fusion.42 = (f32[512]{0:T(512)S(1)}, f32[512]{0:T(512)S(1)}, f32[2048]{0:T(1024)S(1)}) fusion(f32[2048]{0:T(1024)S(1)} %bitcast.119, f32[512]{0:T(512)S(1)} %get-tuple-element.752, f32[512]{0:T(512)S(1)} %get-tuple-element.758, bf16[512,128]{1,0:T(8,128)(2,1)S(1)} %get-tuple-element.757, bf16[8,2048,128]{2,1,0:T(8,128)(2,1)} %get-tuple-element.756, ...), kind=kOutput, calls=%fused_computation.21.clone.1 | convolution fusion | flops 292549632 | bytes 698372 | tf_op jit(solution)/shard_map/while/body/eval_jaxpr/dot_general | solution.py:43
  248.7 6.6 %fusion.42 = (f32[512]{0:T(512)S(1)}, f32[512]{0:T(512)S(1)}, f32[2048]{0:T(1024)S(1)}) fusion(f32[2048]{0:T(1024)S(1)} %bitcast.119, f32[512]{0:T(512)S(1)} %get-tuple-element.752, f32[512]{0:T(512)S(1)} %get-tuple-element.758, bf16[512,128]{1,0:T(8,128)(2,1)S(1)} %get-tuple-element.757, bf16[8,2048,128]{2,1,0:T(8,128)(2,1)} %get-tuple-element.756, ...), kind=kOutput, calls=%fused_computation.21.clone.1 | convolution fusion | flops 292549632 | bytes 698372 | tf_op jit(solution)/shard_map/while/body/eval_jaxpr/dot_general | solution.py:43
  255.6 6.6 %fusion.42 = (f32[512]{0:T(512)S(1)}, f32[512]{0:T(512)S(1)}, f32[2048]{0:T(1024)S(1)}) fusion(f32[2048]{0:T(1024)S(1)} %bitcast.119, f32[512]{0:T(512)S(1)} %get-tuple-element.752, f32[512]{0:T(512)S(1)} %get-tuple-element.758, bf16[512,128]{1,0:T(8,128)(2,1)S(1)} %get-tuple-element.757, bf16[8,2048,128]{2,1,0:T(8,128)(2,1)} %get-tuple-element.756, ...), kind=kOutput, calls=%fused_computation.21.clone.1 | convolution fusion | flops 292549632 | bytes 698372 | tf_op jit(solution)/shard_map/while/body/eval_jaxpr/dot_general | solution.py:43
  262.5 6.6 %fusion.42 = (f32[512]{0:T(512)S(1)}, f32[512]{0:T(512)S(1)}, f32[2048]{0:T(1024)S(1)}) fusion(f32[2048]{0:T(1024)S(1)} %bitcast.119, f32[512]{0:T(512)S(1)} %get-tuple-element.752, f32[512]{0:T(512)S(1)} %get-tuple-element.758, bf16[512,128]{1,0:T(8,128)(2,1)S(1)} %get-tuple-element.757, bf16[8,2048,128]{2,1,0:T(8,128)(2,1)} %get-tuple-element.756, ...), kind=kOutput, calls=%fused_computation.21.clone.1 | convolution fusion | flops 292549632 | bytes 698372 | tf_op jit(solution)/shard_map/while/body/eval_jaxpr/dot_general | solution.py:43
  275.7 63.6 %all-reduce.8.cloned.1.call-done = f32[16384]{0:T(1024)} async-done(((f32[16384]{0:T(1024)}), f32[16384]{0:T(1024)}) %all-reduce.8.cloned.1.call-update) | async-done | bytes 65552 | tf_op jit(solution)/shard_map/psum | solution.py:65
  340.8 55.0 %while.47 = (s32[]{:T(128)}, f32[512]{0:T(512)S(1)}, f32[512]{0:T(512)S(1)}, f32[8,2048]{1,0:T(8,128)S(1)}, f32[512]{0:T(512)S(1)}, /*index=5*/f32[8,2048]{1,0:T...) while((s32[]{:T(128)}, f32[512]{0:T(512)S(1)}, ...), condition=%wide.region_20.21_spmd.clone, body=%wide.region_16.20_spmd.clone.sunk | while | flops 292551680 | bytes 776363 | solution.py:54
  340.9 6.6 %fusion.44 = (f32[512]{0:T(512)S(1)}, f32[512]{0:T(512)S(1)}, f32[2048]{0:T(1024)S(1)}) fusion(f32[2048]{0:T(1024)S(1)} %bitcast.122, f32[512]{0:T(512)S(1)} %get-tuple-element.794, f32[512]{0:T(512)S(1)} %get-tuple-element.800, bf16[512,128]{1,0:T(8,128)(2,1)S(1)} %get-tuple-element.799, bf16[8,2048,128]{2,1,0:T(8,128)(2,1)} %get-tuple-element.798, ...), kind=kOutput, calls=%fused_computation.40.clone.1 | convolution fusion | flops 292549632 | bytes 698372 | tf_op jit(solution)/shard_map/while/body/eval_jaxpr/dot_general | solution.py:43
  347.8 6.6 %fusion.44 = (f32[512]{0:T(512)S(1)}, f32[512]{0:T(512)S(1)}, f32[2048]{0:T(1024)S(1)}) fusion(f32[2048]{0:T(1024)S(1)} %bitcast.122, f32[512]{0:T(512)S(1)} %get-tuple-element.794, f32[512]{0:T(512)S(1)} %get-tuple-element.800, bf16[512,128]{1,0:T(8,128)(2,1)S(1)} %get-tuple-element.799, bf16[8,2048,128]{2,1,0:T(8,128)(2,1)} %get-tuple-element.798, ...), kind=kOutput, calls=%fused_computation.40.clone.1 | convolution fusion | flops 292549632 | bytes 698372 | tf_op jit(solution)/shard_map/while/body/eval_jaxpr/dot_general | solution.py:43
  354.6 6.6 %fusion.44 = (f32[512]{0:T(512)S(1)}, f32[512]{0:T(512)S(1)}, f32[2048]{0:T(1024)S(1)}) fusion(f32[2048]{0:T(1024)S(1)} %bitcast.122, f32[512]{0:T(512)S(1)} %get-tuple-element.794, f32[512]{0:T(512)S(1)} %get-tuple-element.800, bf16[512,128]{1,0:T(8,128)(2,1)S(1)} %get-tuple-element.799, bf16[8,2048,128]{2,1,0:T(8,128)(2,1)} %get-tuple-element.798, ...), kind=kOutput, calls=%fused_computation.40.clone.1 | convolution fusion | flops 292549632 | bytes 698372 | tf_op jit(solution)/shard_map/while/body/eval_jaxpr/dot_general | solution.py:43
  361.5 6.6 %fusion.44 = (f32[512]{0:T(512)S(1)}, f32[512]{0:T(512)S(1)}, f32[2048]{0:T(1024)S(1)}) fusion(f32[2048]{0:T(1024)S(1)} %bitcast.122, f32[512]{0:T(512)S(1)} %get-tuple-element.794, f32[512]{0:T(512)S(1)} %get-tuple-element.800, bf16[512,128]{1,0:T(8,128)(2,1)S(1)} %get-tuple-element.799, bf16[8,2048,128]{2,1,0:T(8,128)(2,1)} %get-tuple-element.798, ...), kind=kOutput, calls=%fused_computation.40.clone.1 | convolution fusion | flops 292549632 | bytes 698372 | tf_op jit(solution)/shard_map/while/body/eval_jaxpr/dot_general | solution.py:43
  368.4 6.6 %fusion.44 = (f32[512]{0:T(512)S(1)}, f32[512]{0:T(512)S(1)}, f32[2048]{0:T(1024)S(1)}) fusion(f32[2048]{0:T(1024)S(1)} %bitcast.122, f32[512]{0:T(512)S(1)} %get-tuple-element.794, f32[512]{0:T(512)S(1)} %get-tuple-element.800, bf16[512,128]{1,0:T(8,128)(2,1)S(1)} %get-tuple-element.799, bf16[8,2048,128]{2,1,0:T(8,128)(2,1)} %get-tuple-element.798, ...), kind=kOutput, calls=%fused_computation.40.clone.1 | convolution fusion | flops 292549632 | bytes 698372 | tf_op jit(solution)/shard_map/while/body/eval_jaxpr/dot_general | solution.py:43
  375.3 6.6 %fusion.44 = (f32[512]{0:T(512)S(1)}, f32[512]{0:T(512)S(1)}, f32[2048]{0:T(1024)S(1)}) fusion(f32[2048]{0:T(1024)S(1)} %bitcast.122, f32[512]{0:T(512)S(1)} %get-tuple-element.794, f32[512]{0:T(512)S(1)} %get-tuple-element.800, bf16[512,128]{1,0:T(8,128)(2,1)S(1)} %get-tuple-element.799, bf16[8,2048,128]{2,1,0:T(8,128)(2,1)} %get-tuple-element.798, ...), kind=kOutput, calls=%fused_computation.40.clone.1 | convolution fusion | flops 292549632 | bytes 698372 | tf_op jit(solution)/shard_map/while/body/eval_jaxpr/dot_general | solution.py:43
  382.1 6.6 %fusion.44 = (f32[512]{0:T(512)S(1)}, f32[512]{0:T(512)S(1)}, f32[2048]{0:T(1024)S(1)}) fusion(f32[2048]{0:T(1024)S(1)} %bitcast.122, f32[512]{0:T(512)S(1)} %get-tuple-element.794, f32[512]{0:T(512)S(1)} %get-tuple-element.800, bf16[512,128]{1,0:T(8,128)(2,1)S(1)} %get-tuple-element.799, bf16[8,2048,128]{2,1,0:T(8,128)(2,1)} %get-tuple-element.798, ...), kind=kOutput, calls=%fused_computation.40.clone.1 | convolution fusion | flops 292549632 | bytes 698372 | tf_op jit(solution)/shard_map/while/body/eval_jaxpr/dot_general | solution.py:43
  389.0 6.6 %fusion.44 = (f32[512]{0:T(512)S(1)}, f32[512]{0:T(512)S(1)}, f32[2048]{0:T(1024)S(1)}) fusion(f32[2048]{0:T(1024)S(1)} %bitcast.122, f32[512]{0:T(512)S(1)} %get-tuple-element.794, f32[512]{0:T(512)S(1)} %get-tuple-element.800, bf16[512,128]{1,0:T(8,128)(2,1)S(1)} %get-tuple-element.799, bf16[8,2048,128]{2,1,0:T(8,128)(2,1)} %get-tuple-element.798, ...), kind=kOutput, calls=%fused_computation.40.clone.1 | convolution fusion | flops 292549632 | bytes 698372 | tf_op jit(solution)/shard_map/while/body/eval_jaxpr/dot_general | solution.py:43
  404.3 21.1 %all-reduce = (f32[]{:T(128)}, f32[]{:T(128)}, f32[]{:T(128)}) all-reduce(f32[]{:T(128)} %get-tuple-element.334, f32[]{:T(128)} %get-tuple-element.335, f32[]{:T(128)} %get-tuple-element.333), channel_id=1, replica_groups=mesh['fac'=8,'cust'=4] {'fac'}, use_global_device_ids=true, to_apply=%region_35.36 | all-reduce | flops 3 | bytes 24 | tf_op jit(solution)/shard_map/psum | solution.py:65
  429.8 36.1 %all-reduce.10.cloned.1.call-done = f32[16384]{0:T(1024)} async-done(((f32[16384]{0:T(1024)}), f32[16384]{0:T(1024)}) %all-reduce.10.cloned.1.call-update) | async-done | bytes 65552 | tf_op jit(solution)/shard_map/psum | solution.py:65
  (174 shorter events, 40.1 us)
Async XLA Ops:
  7.2 82.5 %copy-start.2 = (bf16[512,128]{1,0:T(8,128)(2,1)S(1)}, bf16[512,128]{1,0:T(8,128)(2,1)}, u32[]{:S(2)}) copy-start(bf16[512,128]{1,0:T(8,128)(2,1)} %param.14) | copy-start | bytes 393220
  7.2 82.5 %copy-start.5 = (f32[512]{0:T(512)S(1)}, f32[512]{0:T(512)}, u32[]{:S(2)}) copy-start(f32[512]{0:T(512)} %param.20) | copy-start | bytes 6148
  7.2 78.5 %all-gather.2.cloned.1.call-start = ((), (), s32[]{:S(2)}) async-start(), calls=%async_computation | async-start | bytes 4718592 | tf_op jit(solution)/shard_map/all_gather | solution.py:19
  7.9 205.4 %all-reduce.6.cloned.1.call-start = ((), (), s32[]{:S(2)}) async-start(), calls=%async_computation.1 | async-start | bytes 131072 | tf_op jit(solution)/shard_map/psum | solution.py:65
  89.7 61.5 %copy-start.4 = (f32[512]{0:T(512)S(1)}, f32[512]{0:T(512)}, u32[]{:S(2)}) copy-start(f32[512]{0:T(512)} %param.19) | copy-start | bytes 6148
  89.7 123.7 %copy-start = (s32[16384]{0:T(1024)S(1)}, s32[16384]{0:T(1024)}, u32[]{:S(2)}) copy-start(s32[16384]{0:T(1024)} %param.17) | copy-start | bytes 196612
  89.7 123.7 %copy-start.1 = (f32[16384]{0:T(1024)S(1)}, f32[16384]{0:T(1024)}, u32[]{:S(2)}) copy-start(f32[16384]{0:T(1024)} %param.21) | copy-start | bytes 196612
  145.4 193.9 %all-reduce.8.cloned.1.call-start = ((), (), s32[]{:S(2)}) async-start(), calls=%async_computation.2 | async-start | bytes 131072 | tf_op jit(solution)/shard_map/psum | solution.py:65
  269.9 195.9 %all-reduce.10.cloned.1.call-start = ((), (), s32[]{:S(2)}) async-start(), calls=%async_computation.3 | async-start | bytes 131072 | tf_op jit(solution)/shard_map/psum | solution.py:65
  340.8 55.7 %copy-start.3 = (s32[512]{0:T(512)S(1)}, s32[512]{0:T(512)}, u32[]{:S(2)}) copy-start(s32[512]{0:T(512)} %param.16) | copy-start | bytes 6148
  340.8 62.2 %copy-start.6 = (f32[512]{0:T(512)S(1)}, f32[512]{0:T(512)}, u32[]{:S(2)}) copy-start(f32[512]{0:T(512)} %param.18) | copy-start | bytes 6148
Sparse Core Ops, SparseCore 0:
  10.1 75.5 all-gather.1
  145.5 67.7 all-reduce.5
  270.0 69.1 all-reduce.7
  396.6 69.2 all-reduce.9
where the time goes:
time: 475 us; the launch traced here: 474 us
  waiting for transfers between devices  237 us (50%)
  matrix products  157 us (33%)
  blocking collectives  39 us (8%)
  between operations  17.7 us (4%)
  other arithmetic  12.6 us (3%)
  local copies, waits for them, and re-layouts  8.74 us (2%)
    psum x3, waiting for transfers between devices, local(): cover, row_sum = lax.psum((cover_part, row_total), 'fac')  162 us
    dot_general x24, matrix products, one_block(): lax.dot_general(fac_coords, cols, (((1,), (1,)), ((), ())), preferred_ele...  157 us
    all_gather x1, waiting for transfers between devices, local(): coords_all = lax.all_gather(cust_coords, 'fac', axis=0, tiled=True)  74.2 us
    psum x1, blocking collectives, local(): cover, row_sum = lax.psum((cover_part, row_total), 'fac')  21.1 us
    psum x3, blocking collectives, local(): load, soft, lam_total = lax.psum((carry[0], soft_part, lam_local), 'cust')  17.9 us
  transfers between devices with their start and end apart: 4, of which 4 were waited for; matrix products, arithmetic and copies ran while one was open for 1% of the time, Pallas kernels for 0%

commit v1 on v0

v1 whole, which is shorter than its diff:
```python
import functools
import math

import jax
import jax.numpy as jnp
from jax import lax
from jax.experimental import pallas as pl
from jax.experimental.pallas import tpu as pltpu
from jax.sharding import PartitionSpec as P

MESH = pl.DeviceIdType.MESH
ITERS = 3
TAU = 0.1
ALIGN = 16
ROWS = 256
F32 = jnp.float32
BF16 = jnp.bfloat16
VMEM = pl.BlockSpec(memory_space=pltpu.VMEM)


def split3(v):
    a = v.astype(BF16)
    r = v - a.astype(F32)
    b = r.astype(BF16)
    c = (r - b.astype(F32)).astype(BF16)
    return a, b, c


def onehot_of(open_row):
    n = open_row.shape[1]
    flags = jnp.broadcast_to(open_row.astype(F32), (16, n)).astype(BF16)
    tri = (lax.broadcasted_iota(jnp.int32, (n, n), 0) <= lax.broadcasted_iota(jnp.int32, (n, n), 1)).astype(F32).astype(BF16)
    pos = jnp.dot(flags, tri, preferred_element_type=F32)[0:1]
    pos = jnp.where(open_row > 0, pos - 1.0, -1.0).astype(jnp.int32)
    hit = lax.broadcasted_iota(jnp.int32, (n, n), 0) == pos
    return jnp.where(hit, 1.0, 0.0).astype(BF16)


def nt(a, b):
    return lax.dot_general(a, b, (((1,), (1,)), ((), ())), preferred_element_type=F32)


def pre_kernel(open_ref, fac_ref, cap_ref, mu_ref, cust_ref, comp_ref, info_ref, cust_t_ref, hq_ref):
    n, width = fac_ref.shape
    hot = onehot_of(open_ref[...])
    fac = fac_ref[...]
    comp_ref[...] = jnp.dot(hot, fac, preferred_element_type=F32).astype(BF16)
    sq = fac.astype(F32) ** 2
    s1, s2, _ = split3(sq)
    ones = jnp.ones((16, width), BF16)
    half = -0.5 * (nt(ones, s1) + nt(ones, s2))[0:1]
    rows = [jnp.ones((1, n), BF16)]
    for v in (half, mu_ref[...], cap_ref[...]):
        rows.extend(split3(v))
    rows = [r.astype(F32) for r in rows] + [jnp.zeros((6, n), F32)]
    got = nt(jnp.concatenate(rows, axis=0).astype(BF16), hot)
    info_ref[0:1, :] = got[0:1]
    for m in range(3):
        info_ref[m + 1:m + 2, :] = got[3 * m + 1:3 * m + 2] + got[3 * m + 2:3 * m + 3] + got[3 * m + 3:3 * m + 4]
    info_ref[4:8, :] = jnp.zeros((4, n), F32)
    eye = (lax.broadcasted_iota(jnp.int32, (width, width), 0) == lax.broadcasted_iota(jnp.int32, (width, width), 1)).astype(F32).astype(BF16)
    turned = nt(eye, cust_ref[...])
    cust_t_ref[...] = turned.astype(BF16)
    hq_ref[...] = 0.5 * jnp.sum(turned * turned, axis=0, keepdims=True)


def sync(peers):
    barrier = pltpu.get_barrier_semaphore()
    for peer in peers:
        pl.semaphore_signal(barrier, inc=1, device_id=peer, device_id_type=MESH)
    pl.semaphore_wait(barrier, len(peers))


def gather_kernel(nf, nc, comp_ref, info_ref, facs_ref, infos_ref, s1, r1, s2, r2, s3, r3, loc):
    f, c = lax.axis_index("fac"), lax.axis_index("cust")
    fp = [(lax.rem(f + d, nf), c) for d in range(1, nf)]
    cp = [(f, lax.rem(c + d, nc)) for d in range(1, nc)]
    n = comp_ref.shape[0]
    part = n // nc
    sync(fp + cp)
    mine = pl.ds(pl.multiple_of(c * part, part), part)
    own = pltpu.make_async_copy(comp_ref, facs_ref.at[f], loc.at[0])
    own.start()
    own_info = pltpu.make_async_copy(info_ref, infos_ref.at[f], loc.at[1])
    own_info.start()
    sends = []
    for d, peer in enumerate(fp):
        cpy = pltpu.make_async_remote_copy(comp_ref.at[mine], facs_ref.at[f, mine], s1.at[d], r1.at[d], device_id=peer, device_id_type=MESH)
        cpy.start()
        sends.append(cpy)
        cpy = pltpu.make_async_remote_copy(info_ref, infos_ref.at[f], s3.at[d], r3.at[d], device_id=peer, device_id_type=MESH)
        cpy.start()
        sends.append(cpy)
    seconds = []
    for d in range(nf - 1):
        src = lax.rem(f + nf - 1 - d, nf)
        sends[2 * d].wait_recv()
        for e, peer in enumerate(cp):
            cpy = pltpu.make_async_remote_copy(facs_ref.at[src, mine], facs_ref.at[src, mine], s2.at[d, e], r2.at[d, e], device_id=peer, device_id_type=MESH)
            cpy.start()
            seconds.append(cpy)
    for d in range(nf - 1):
        sends[2 * d].wait_send()
        sends[2 * d + 1].wait()
    for cpy in seconds:
        cpy.wait()
    own.wait()
    own_info.wait()


def step_kernel(first, size, prev, facs_ref, info_ref, mu_ref, load_ref, cust_t_ref, hq_ref, lam_ref, wt_ref,
                part_ref, mu_out_ref, lam_out_ref, tot_ref,
                a_ref, w_ref, y_ref, acc_ref, cov_ref, soft_ref):
    nf, n, width = facs_ref.shape
    cols = cust_t_ref.shape[1]
    block = y_ref.shape[2]
    tiles = cols // block
    lam = lam_ref[...]
    wt = wt_ref[...]
    a1, a2, a3 = split3(64.0 * lam - hq_ref[...])
    one_c = jnp.ones((3, cols), F32)
    mw = jnp.broadcast_to(-64.0 * wt, (3, cols))
    aug = jnp.concatenate([a1.astype(F32), a2.astype(F32), a3.astype(F32), one_c, mw, jnp.zeros((7, cols), F32)], axis=0)
    w_ref[0:width, :] = cust_t_ref[...]
    w_ref[width:width + 16, :] = aug.astype(BF16)
    w_ref[width + 16:, :] = jnp.zeros((width - 16, cols), BF16)
    cov_ref[...] = jnp.zeros_like(cov_ref)
    soft_ref[...] = jnp.zeros_like(soft_ref)
    lane = lax.broadcasted_iota(jnp.int32, (ROWS, width), 1)
    pad = jnp.where(lane == 3, -30000.0, 0.0).astype(BF16)
    sel = (lax.broadcasted_iota(jnp.int32, (16, width), 0) == lax.broadcasted_iota(jnp.int32, (16, width), 1)).astype(F32).astype(BF16)
    offs = []
    off = jnp.int32(0)
    one_r = jnp.ones((3, n), F32)
    for f in range(nf):
        valid = info_ref[f, 0:1, :]
        cap = info_ref[f, 3:4, :]
        if first:
            mu = info_ref[f, 2:3, :]
        else:
            mu = mu_ref[f:f + 1, :]
            load = load_ref[f:f + 1, :]
            mu = jnp.maximum(0.0, mu + prev * (load - cap) / (load + jnp.where(valid > 0, cap, 1.0)))
        mu = mu * valid
        mu_out_ref[f:f + 1, :] = mu
        b = jnp.where(valid > 0, info_ref[f, 1:2, :], -30000.0)
        parts = [p.astype(F32) for p in split3(b) + split3(mu)]
        rows = jnp.concatenate([one_r] + parts + [jnp.zeros((7, n), F32)], axis=0).astype(BF16)
        side = lax.dot_general(rows, sel, (((0,), (0,)), ((), ())), preferred_element_type=F32).astype(BF16)
        count = jnp.sum(valid).astype(jnp.int32)
        off = pl.multiple_of(off, ALIGN)
        offs.append(off)
        a_ref[pl.ds(off, n), 0:width] = facs_ref[f]
        a_ref[pl.ds(off, n), width:2 * width] = side
        off = off + ((count + ALIGN - 1) // ALIGN) * ALIGN
    tail = pl.multiple_of(off, ALIGN)
    a_ref[pl.ds(tail, ROWS), 0:width] = jnp.zeros((ROWS, width), BF16)
    a_ref[pl.ds(tail, ROWS), width:2 * width] = pad
    n_blocks = (off + ROWS - 1) // ROWS
    scale = math.log2(math.e) / 6.4

    def body(i, _):
        base = pl.multiple_of(i * ROWS, ROWS)
        lhs = a_ref[pl.ds(base, ROWS), :]

        def dot(t):
            y_ref[t % 2] = jnp.dot(lhs, w_ref[:, t * block:(t + 1) * block], preferred_element_type=F32)

        dot(0)
        for t in range(tiles):
            if t + 1 < tiles:
                dot(t + 1)
            covs = [cov_ref[:, t * block + q * 128:t * block + (q + 1) * 128] for q in range(block // 128)]
            softs = [soft_ref[:, t * block + q * 128:t * block + (q + 1) * 128] for q in range(block // 128)]
            for r in range(0, ROWS, 32):
                loads = [None] * 4
                for q in range(block // 128):
                    at = t * block + q * 128
                    wq = jnp.broadcast_to(wt_ref[:, at:at + 128], (8, 128))
                    es = [jnp.exp2(y_ref[t % 2, r + 8 * s:r + 8 * s + 8, q * 128:(q + 1) * 128] * scale) for s in range(4)]
                    us = [1.0 + e for e in es]
                    p01 = us[0] * us[1]
                    p23 = us[2] * us[3]
                    r01 = 1.0 / p01
                    r23 = 1.0 / p23
                    xs = [es[0] * (us[1] * r01), es[1] * (us[0] * r01), es[2] * (us[3] * r23), es[3] * (us[2] * r23)]
                    covs[q] = covs[q] + ((xs[0] + xs[1]) + (xs[2] + xs[3]))
                    softs[q] = softs[q] + jnp.log(p01 * p23)
                    for s in range(4):
                        v = xs[s] * wq
                        loads[s] = v if loads[s] is None else loads[s] + v
                for s in range(4):
                    at = pl.ds(base + r + 8 * s, 8)
                    if t == 0:
                        acc_ref[at, :] = loads[s]
                    else:
                        acc_ref[at, :] = acc_ref[at, :] + loads[s]
            for q in range(block // 128):
                cov_ref[:, t * block + q * 128:t * block + (q + 1) * 128] = covs[q]
                soft_ref[:, t * block + q * 128:t * block + (q + 1) * 128] = softs[q]
        return 0

    lax.fori_loop(0, n_blocks, body, 0)
    ones = jnp.ones((8, 128), F32)
    for f in range(nf):
        got = lax.dot_general(ones, acc_ref[pl.ds(offs[f], n), :], (((1,), (1,)), ((), ())), preferred_element_type=F32, precision=lax.Precision.HIGHEST)
        part_ref[f:f + 1, :] = jnp.where(info_ref[f, 0:1, :] > 0, got[0:1], 0.0)
    cover = jnp.sum(cov_ref[...], axis=0, keepdims=True)
    soft = jnp.sum(soft_ref[...], axis=0, keepdims=True)
    tot_ref[...] = jnp.full((8, 128), jnp.sum(wt * lam - TAU * wt * soft), F32)
    lam_out_ref[...] = lam + size * wt * (1.0 - cover) / (1.0 + cover)


def exchange(peers, src, slots, send, recv):
    copies = []
    for d, peer in enumerate(peers):
        cpy = pltpu.make_async_remote_copy(src, slots.at[d], send.at[d], recv.at[d], device_id=peer, device_id_type=MESH)
        cpy.start()
        copies.append(cpy)
    return copies


def reduce_kernel(nf, nc, x_ref, out_ref, got1, mid, got2, s1, r1, s2, r2):
    f, c = lax.axis_index("fac"), lax.axis_index("cust")
    fp = [(lax.rem(f + d, nf), c) for d in range(1, nf)]
    cp = [(f, lax.rem(c + d, nc)) for d in range(1, nc)]
    sync(fp + cp)
    first = exchange(cp, x_ref, got1, s1, r1)
    total = x_ref[...]
    for d, cpy in enumerate(first):
        cpy.wait()
        total = total + got1[d]
    mid[...] = total
    second = exchange(fp, mid, got2, s2, r2)
    for d, cpy in enumerate(second):
        cpy.wait()
        total = total + got2[d]
    out_ref[...] = total


def gather_lam_kernel(nf, lam_ref, out_ref, s1, r1, loc):
    f, c = lax.axis_index("fac"), lax.axis_index("cust")
    fp = [(lax.rem(f + d, nf), c) for d in range(1, nf)]
    sync(fp)
    own = pltpu.make_async_copy(lam_ref, out_ref.at[f], loc)
    own.start()
    copies = []
    for d, peer in enumerate(fp):
        cpy = pltpu.make_async_remote_copy(lam_ref, out_ref.at[f], s1.at[d], r1.at[d], device_id=peer, device_id_type=MESH)
        cpy.start()
        copies.append(cpy)
    for cpy in copies:
        cpy.wait()
    own.wait()


def params(cid=None, mib=56):
    return pltpu.CompilerParams(collective_id=cid, has_side_effects=True, vmem_limit_bytes=mib * 2 ** 20) if cid is not None else pltpu.CompilerParams(vmem_limit_bytes=mib * 2 ** 20)


def local(nf, nc, fac_coords, cust_coords, open_flags, demand, fixed_cost, capacity, cap_mult, cover_mult):
    n, width = fac_coords.shape
    cols = cust_coords.shape[0]
    total_cust = cols * nf * nc
    f = lax.axis_index("fac")
    c = lax.axis_index("cust")
    sd = jax.ShapeDtypeStruct
    dma = pltpu.SemaphoreType.DMA
    wt = lax.dynamic_slice_in_dim(demand, f * cols, cols).astype(F32).reshape(1, cols)
    lam = lax.dynamic_slice_in_dim(cover_mult, f * cols, cols).reshape(1, cols)
    open_row = open_flags.reshape(1, n)
    comp, info, cust_t, hq = pl.pallas_call(
        pre_kernel,
        out_shape=(sd((n, width), BF16), sd((8, n), F32), sd((width, cols), BF16), sd((1, cols), F32)),
        in_specs=[VMEM] * 5, out_specs=(VMEM,) * 4, compiler_params=params(), name="pre",
    )(open_row, fac_coords, capacity.reshape(1, n), cap_mult.reshape(1, n), cust_coords)
    facs, infos = pl.pallas_call(
        functools.partial(gather_kernel, nf, nc),
        out_shape=(sd((nf, n, width), BF16), sd((nf, 8, n), F32)),
        in_specs=[VMEM] * 2, out_specs=(VMEM,) * 2,
        scratch_shapes=[dma((nf - 1,)), dma((nf - 1,)), dma((nf - 1, nc - 1)), dma((nf - 1, nc - 1)), dma((nf - 1,)), dma((nf - 1,)), dma((2,))],
        compiler_params=params(0), name="gather",
    )(comp, info)
    block = math.gcd(cols, 512)
    total_rows = nf * n
    tots = []
    mus = []
    mu = load = jnp.zeros((nf, n), F32)
    for step in range(ITERS):
        part, mu, lam, tot = pl.pallas_call(
            functools.partial(step_kernel, step == 0, 0.1 / (step + 1), 0.1 / max(step, 1)),
            out_shape=(sd((nf, n), F32), sd((nf, n), F32), sd((1, cols), F32), sd((8, 128), F32)),
            in_specs=[VMEM] * 8, out_specs=(VMEM,) * 4,
            scratch_shapes=[
                pltpu.VMEM((total_rows + n + ROWS, 2 * width), BF16),
                pltpu.VMEM((2 * width, cols), BF16),
                pltpu.VMEM((2, ROWS, block), F32),
                pltpu.VMEM((total_rows + n + ROWS, 128), F32),
                pltpu.VMEM((8, cols), F32),
                pltpu.VMEM((8, cols), F32),
            ],
            compiler_params=params(), name="step",
        )(facs, infos, mu, load, cust_t, hq, lam, wt)
        mus.append(mu)
        tots.append(tot[0, 0])
        payload = part
        if step == ITERS - 1:
            opened = open_flags.astype(F32)
            shut = cap_mult
            extras = []
            for k in range(ITERS):
                fixed = jnp.sum(opened * fixed_cost - (1.0 - opened) * shut * capacity)
                mine = jnp.sum(mus[k] * jnp.where(lax.broadcasted_iota(jnp.int32, (nf, n), 0) == f, infos[:, 3, :], 0.0))
                extras.append(tots[k] + jnp.where(c == 0, fixed - mine, 0.0))
                shut = jnp.maximum(0.0, shut - 0.1 / (k + 1))
            row = jnp.concatenate([jnp.stack(extras), jnp.zeros((n - ITERS,), F32)])
            payload = jnp.concatenate([part, row[None], jnp.zeros((7, n), F32)], axis=0)
        rows = payload.shape[0]
        load = pl.pallas_call(
            functools.partial(reduce_kernel, nf, nc),
            out_shape=sd((rows, n), F32), in_specs=[VMEM], out_specs=VMEM,
            scratch_shapes=[pltpu.VMEM((nc - 1, rows, n), F32), pltpu.VMEM((rows, n), F32), pltpu.VMEM((nf - 1, rows, n), F32),
                            dma((nc - 1,)), dma((nc - 1,)), dma((nf - 1,)), dma((nf - 1,))],
            compiler_params=params(1 + step), name="reduce",
        )(payload)
    lam_all = pl.pallas_call(
        functools.partial(gather_lam_kernel, nf),
        out_shape=sd((nf, 1, cols), F32), in_specs=[VMEM], out_specs=VMEM,
        scratch_shapes=[dma((nf - 1,)), dma((nf - 1,)), dma(())],
        compiler_params=params(1 + ITERS), name="lams",
    )(lam)
    bounds = load[nf, 0:ITERS] / total_cust
    total = lax.dynamic_slice_in_dim(load, f, 1, 0)
    cap = lax.dynamic_slice_in_dim(infos, f, 1, 0)[0, 3:4]
    last = lax.dynamic_slice_in_dim(mu, f, 1, 0)

    def finish(total_ref, last_ref, cap_ref, open_ref, shut_ref, out_ref):
        load, cap = total_ref[...], cap_ref[...]
        new = jnp.maximum(0.0, last_ref[...] + (0.1 / ITERS) * (load - cap) / (load + jnp.where(cap > 0, cap, 1.0)))
        hot = onehot_of(open_ref[...])
        rows = jnp.concatenate([v.astype(F32) for v in split3(new)] + [jnp.zeros((13, n), F32)], axis=0).astype(BF16)
        got = jnp.dot(rows, hot, preferred_element_type=F32)
        out_ref[...] = jnp.where(open_ref[...] > 0, got[0:1] + got[1:2] + got[2:3], shut_ref[...])

    cap_final = pl.pallas_call(finish, out_shape=sd((1, n), F32), in_specs=[VMEM] * 5, out_specs=VMEM, compiler_params=params(), name="finish")(
        total, last, cap, open_row, shut.reshape(1, n))
    return lam_all.reshape(nf * cols), cap_final.reshape(n), bounds


def solution(mesh):
    nf, nc = mesh.shape["fac"], mesh.shape["cust"]
    return jax.shard_map(
        functools.partial(local, nf, nc),
        mesh=mesh,
        in_specs=(P("fac", None), P(("cust", "fac"), None), P("fac"), P("cust"), P("fac"), P("fac"), P("fac"), P("cust")),
        out_specs=(P("cust"), P("fac"), P()),
        check_vma=False,
    )
```

time: 475 us -> 137 us (0.29)
  waiting for transfers between devices: 237 us -> 0 us
  matrix products: 157 us -> 0 us
  Pallas kernels: 0 us -> 115 us
  blocking collectives: 39 us -> 0 us
  between operations: 17.7 us -> 6.38 us
  other arithmetic: 12.6 us -> 5.25 us
    psum x3 -> x0, waiting for transfers between devices: 162 us -> none  [local(): cover, row_sum = lax.psum((cover_part, row_total), 'fac')]
    dot_general x24 -> x0, matrix products: 157 us -> none  [one_block(): lax.dot_general(fac_coords, cols, (((1,), (1,)), ((), ())), preferred_ele...]
    pallas_call x0 -> x10, Pallas kernels: none -> 115 us  [the longest x3 41.9 us: local(): pl.pallas_call(functools.partial(step_kernel, step == 0, 0.1 / (step + 1)...]
    all_gather x1 -> x0, waiting for transfers between devices: 74.2 us -> none  [local(): coords_all = lax.all_gather(cust_coords, 'fac', axis=0, tiled=True)]
    psum x4 -> x0, blocking collectives: 39 us -> none  [the longest x1 21.1 us: local(): cover, row_sum = lax.psum((cover_part, row_total), 'fac')]
    reduce_sum x4 -> x2, other arithmetic: 7.71 us -> 1.98 us  [the longest x1 1.28 us: local(): fixed = jnp.sum(opened * fixed_cost - (1.0 - opened) * shut * capacity)]
    dynamic_update_slice x24 -> x0, local copies, waits for them, and re-layouts: 4.88 us -> none  [local(): lax.scan(one_block, (zeros_rows, zeros_rows), (coord_blocks, qnorm_blocks...]
  transfers between devices with their start and end apart: 4 -> 0, of which waited for: 4 -> 0; matrix products, arithmetic and copies ran while one was open for 1% -> 0% of each run, Pallas kernels for 0% -> 0%
where the time goes in v1:
time: 137 us; the launch traced here: 136 us
  Pallas kernels  115 us (84%)
  local copies, waits for them, and re-layouts  9.55 us (7%)
  between operations  6.38 us (5%)
  other arithmetic  5.25 us (4%)
    pallas_call x3, Pallas kernels, local(): pl.pallas_call(functools.partial(step_kernel, step == 0, 0.1 / (step + 1)...  41.9 us
    pallas_call x3, Pallas kernels, local(): pl.pallas_call(functools.partial(reduce_kernel, nf, nc), out_shape=sd((ro...  37.7 us
    pallas_call x1, Pallas kernels, local(): pl.pallas_call(functools.partial(gather_kernel, nf, nc), out_shape=(sd((n...  22.5 us
    pallas_call x1, Pallas kernels, local(): pl.pallas_call(functools.partial(gather_lam_kernel, nf), out_shape=sd((nf...  8.3 us
    slice x3, local copies, waits for them, and re-layouts, local(): tots.append(tot[0, 0])  3.58 us
    pallas_call x1, Pallas kernels, local(): pl.pallas_call(pre_kernel, out_shape=(sd((n, width), BF16), sd((8, n), F3...  2.78 us

profile of v1, /device:TPU:0, one launch (start us, length us, event | category | flops | bytes accessed | tf_op | source)
XLA Modules:
  0.0 136.0 jit_solution(2716046700794888488)
XLA Ops:
  0.6 2.8 %pre.1 = (bf16[512,128]{1,0:T(8,128)(2,1)}, f32[8,512]{1,0:T(8,128)}, bf16[128,2048]{1,0:T(8,128)(2,1)}, f32[1,2048]{1,0:T(1,128)}) custom-call(s32[1,512]{1,0:T(1,128)} %bitcast.34, bf16[512,128]{1,0:T(8,128)(2,1)} %fac_ref.1, f32[1,512]{1,0:T(1,128)} %bitcast.36, f32[1,512]{1,0:T(1,128)} %bitcast.37, bf16[2048,128]{1,0:T(8,128)(2,1)} %cust_ref.1), custom_call_target="tpu_custom_call" | custom-call | tf_op jit(solution)/shard_map/pre/pallas_call | solution.py:272
  3.4 22.5 %gather.1 = (bf16[8,512,128]{2,1,0:T(8,128)(2,1)}, f32[8,8,512]{2,1,0:T(8,128)}) custom-call(bf16[512,128]{1,0:T(8,128)(2,1)} %get-tuple-element.21.comp_ref, f32[8,512]{1,0:T(8,128)} %get-tuple-element.22.info_ref), custom_call_target="tpu_custom_call" | custom-call | tf_op jit(solution)/shard_map/gather/pallas_call | solution.py:277
  25.9 1.3 dynamic_slice.15
  27.2 1.3 dynamic-slice_convert_fusion
  28.5 0.6 broadcast_in_dim.16.mu_ref.load_ref
  29.1 13.9 %step.3 = (f32[8,512]{1,0:T(8,128)}, f32[8,512]{1,0:T(8,128)}, f32[1,2048]{1,0:T(1,128)}, f32[8,128]{1,0:T(8,128)}) custom-call(bf16[8,512,128]{2,1,0:T(8,128)(2,1)} %get-tuple-element.23.facs_ref, f32[8,8,512]{2,1,0:T(8,128)} %get-tuple-element.24.info_ref, f32[8,512]{1,0:T(8,128)} %broadcast_in_dim.16.mu_ref.load_ref, ...), custom_call_target="tpu_custom_call" | custom-call | tf_op jit(solution)/shard_map/step/pallas_call | solution.py:290
  43.0 11.7 %reduce.3.load_ref = f32[8,512]{1,0:T(8,128)} custom-call(f32[8,512]{1,0:T(8,128)} %get-tuple-element.28.x_ref), custom_call_target="tpu_custom_call" | custom-call | tf_op jit(solution)/shard_map/reduce/pallas_call | solution.py:319
  54.7 14.0 %step.4 = (f32[8,512]{1,0:T(8,128)}, f32[8,512]{1,0:T(8,128)}, f32[1,2048]{1,0:T(1,128)}, f32[8,128]{1,0:T(8,128)}) custom-call(bf16[8,512,128]{2,1,0:T(8,128)(2,1)} %get-tuple-element.23.facs_ref, f32[8,8,512]{2,1,0:T(8,128)} %get-tuple-element.24.info_ref, f32[8,512]{1,0:T(8,128)} %get-tuple-element.27.mu_ref, f32[8,512]{1,0:T(8,128)} %reduce.3.load_ref, ...), custom_call_target="tpu_custom_call" | custom-call | tf_op jit(solution)/shard_map/step/pallas_call | solution.py:290
  68.7 12.2 %reduce.4.load_ref = f32[8,512]{1,0:T(8,128)} custom-call(f32[8,512]{1,0:T(8,128)} %get-tuple-element.31.x_ref), custom_call_target="tpu_custom_call" | custom-call | tf_op jit(solution)/shard_map/reduce/pallas_call | solution.py:319
  80.9 14.0 %step.5 = (f32[8,512]{1,0:T(8,128)}, f32[8,512]{1,0:T(8,128)}, f32[1,2048]{1,0:T(1,128)}, f32[8,128]{1,0:T(8,128)}) custom-call(bf16[8,512,128]{2,1,0:T(8,128)(2,1)} %get-tuple-element.23.facs_ref, f32[8,8,512]{2,1,0:T(8,128)} %get-tuple-element.24.info_ref, f32[8,512]{1,0:T(8,128)} %get-tuple-element.30.mu_ref, f32[8,512]{1,0:T(8,128)} %reduce.4.load_ref, ...), custom_call_target="tpu_custom_call" | custom-call | tf_op jit(solution)/shard_map/step/pallas_call | solution.py:290
  94.9 8.3 %lams.1 = f32[8,1,2048]{2,1,0:T(1,128)} custom-call(f32[1,2048]{1,0:T(1,128)} %get-tuple-element.33.lam_ref), custom_call_target="tpu_custom_call" | custom-call | tf_op jit(solution)/shard_map/lams/pallas_call | solution.py:326
  103.2 1.2 slice.23
  104.4 0.7 copy-done.7
  105.0 0.0 copy-done.5
  105.1 1.3 subtract_reduce_fusion.2
  106.3 0.1 copy.11
  106.4 0.6 copy-done.2
  107.1 0.0 copy-done.3
  107.1 0.0 copy-done.4
  107.1 0.7 multiply_reduce_fusion.2
  109.8 1.2 slice.22
  112.8 0.0 copy-start.6
  112.8 1.2 slice.20
  115.9 0.1 pad_maximum_fusion
  115.9 0.1 pad.2.clone
  116.0 0.7 maximum_maximum_fusion.x_ref
  116.7 13.8 %reduce.5 = f32[16,512]{1,0:T(8,128)} custom-call(f32[16,512]{1,0:T(8,128)} %maximum_maximum_fusion.x_ref), custom_call_target="tpu_custom_call" | custom-call | tf_op jit(solution)/shard_map/reduce/pallas_call | solution.py:319
  130.5 1.3 constant_dynamic-slice_fusion
  131.9 0.6 dynamic-slice_bitcast_fusion.cap_ref
  132.4 1.7 %finish.1 = f32[1,512]{1,0:T(1,128)} custom-call(f32[1,512]{1,0:T(1,128)} %get-tuple-element.47.total_ref, f32[1,512]{1,0:T(1,128)} %get-tuple-element.46.last_ref, f32[1,512]{1,0:T(1,128)} %dynamic-slice_bitcast_fusion.cap_ref, s32[1,512]{1,0:T(1,128)} %bitcast.35, f32[1,512]{1,0:T(1,128)} %bitcast.39), custom_call_target="tpu_custom_call" | custom-call | tf_op jit(solution)/shard_map/finish/pallas_call | solution.py:345
  134.1 1.2 multiply_bitcast_fusion
  135.3 0.6 copy.13
  (17 shorter events, 0.0 us)
Async XLA Ops:
  80.9 25.5 %copy-start = (f32[8,8,512]{2,1,0:T(8,128)S(1)}, f32[8,8,512]{2,1,0:T(8,128)}, u32[]{:S(2)}) copy-start(f32[8,8,512]{2,1,0:T(8,128)} %get-tuple-element.24.info_ref) | copy-start | bytes 393220
  94.9 9.5 %copy-start.8 = (f32[512]{0:T(512)S(1)}, f32[512]{0:T(512)}, u32[]{:S(2)}) copy-start(f32[512]{0:T(512)} %param.14) | copy-start | bytes 6148
  94.9 9.5 %copy-start.9 = (f32[512]{0:T(512)S(1)}, f32[512]{0:T(512)}, u32[]{:S(2)}) copy-start(f32[512]{0:T(512)} %param.12) | copy-start | bytes 6148
  104.4 0.7 copy-start.7
  104.4 0.7 copy-start.5
  106.3 0.7 copy-start.2
  106.3 0.7 copy-start.3
  106.3 0.7 copy-start.4
  112.8 3.2 %copy-start.6 = (f32[8,512]{1,0:T(8,128)S(1)}, f32[8,512]{1,0:T(8,128)}, u32[]{:S(2)}) copy-start(f32[8,512]{1,0:T(8,128)} %get-tuple-element.34) | copy-start | bytes 49156
  116.7 18.6 %copy-start.1 = (f32[8,1,2048]{2,1,0:T(1,128)S(1)}, f32[8,1,2048]{2,1,0:T(1,128)}, u32[]{:S(2)}) copy-start(f32[8,1,2048]{2,1,0:T(1,128)} %lams.1) | copy-start | bytes 196612

commit v2 on v1

v2 whole, which is shorter than its diff:
```python
import functools
import math

import jax
import jax.numpy as jnp
from jax import lax
from jax.experimental import pallas as pl
from jax.experimental.pallas import tpu as pltpu
from jax.sharding import PartitionSpec as P

MESH = pl.DeviceIdType.MESH
ITERS = 3
TAU = 0.1
ALIGN = 16
ROWS = 256
F32 = jnp.float32
BF16 = jnp.bfloat16
VMEM = pl.BlockSpec(memory_space=pltpu.VMEM)


def split3(v):
    a = v.astype(BF16)
    r = v - a.astype(F32)
    b = r.astype(BF16)
    c = (r - b.astype(F32)).astype(BF16)
    return a, b, c


def onehot_of(open_row):
    n = open_row.shape[1]
    flags = jnp.broadcast_to(open_row.astype(F32), (16, n)).astype(BF16)
    tri = (lax.broadcasted_iota(jnp.int32, (n, n), 0) <= lax.broadcasted_iota(jnp.int32, (n, n), 1)).astype(F32).astype(BF16)
    pos = jnp.dot(flags, tri, preferred_element_type=F32)[0:1]
    pos = jnp.where(open_row > 0, pos - 1.0, -1.0).astype(jnp.int32)
    hit = lax.broadcasted_iota(jnp.int32, (n, n), 0) == pos
    return jnp.where(hit, 1.0, 0.0).astype(BF16)


def nt(a, b):
    return lax.dot_general(a, b, (((1,), (1,)), ((), ())), preferred_element_type=F32)


def pre_kernel(open_ref, fac_ref, cap_ref, mu_ref, fixed_ref, cust_ref, demand_ref, cover_ref,
               comp_ref, info_ref, cust_t_ref, hq_ref, wt_ref, lam_ref, ext_ref, shut_ref):
    n, width = fac_ref.shape
    cols = cust_ref.shape[0]
    nc, _, part = info_ref.shape
    f, c = lax.axis_index("fac"), lax.axis_index("cust")
    mine = pl.ds(pl.multiple_of(f * cols, cols), cols)
    wt_ref[...] = demand_ref[:, mine].astype(F32)
    lam_ref[...] = cover_ref[:, mine]
    opened = open_ref[...].astype(F32)
    shut = mu_ref[...]
    ext = jnp.zeros((8, 128), F32)
    lane = lax.broadcasted_iota(jnp.int32, (8, 128), 1)
    for k in range(ITERS):
        fixed = jnp.sum(opened * fixed_ref[...] - (1.0 - opened) * shut * cap_ref[...])
        ext = ext + jnp.where((lane == k) & (c == 0), fixed, 0.0)
        shut = jnp.maximum(0.0, shut - 0.1 / (k + 1))
    ext_ref[...] = ext
    shut_ref[...] = shut
    hot = onehot_of(open_ref[...])
    fac = fac_ref[...]
    comp_ref[...] = jnp.dot(hot, fac, preferred_element_type=F32).astype(BF16)
    sq = fac.astype(F32) ** 2
    s1, s2, _ = split3(sq)
    ones = jnp.ones((16, width), BF16)
    half = -0.5 * (nt(ones, s1) + nt(ones, s2))[0:1]
    rows = [jnp.ones((1, n), BF16)]
    for v in (half, mu_ref[...], cap_ref[...]):
        rows.extend(split3(v))
    rows = [r.astype(F32) for r in rows] + [jnp.zeros((6, n), F32)]
    got = nt(jnp.concatenate(rows, axis=0).astype(BF16), hot)
    rows = [got[0:1]] + [got[3 * m + 1:3 * m + 2] + got[3 * m + 2:3 * m + 3] + got[3 * m + 3:3 * m + 4] for m in range(3)]
    info = jnp.concatenate(rows + [jnp.zeros((4, n), F32)], axis=0)
    for p in range(nc):
        info_ref[p] = info[:, p * part:(p + 1) * part]
    eye = (lax.broadcasted_iota(jnp.int32, (width, width), 0) == lax.broadcasted_iota(jnp.int32, (width, width), 1)).astype(F32).astype(BF16)
    turned = nt(eye, cust_ref[...])
    cust_t_ref[...] = turned.astype(BF16)
    hq_ref[...] = 0.5 * jnp.sum(turned * turned, axis=0, keepdims=True)


def sync(peers):
    barrier = pltpu.get_barrier_semaphore()
    for peer in peers:
        pl.semaphore_signal(barrier, inc=1, device_id=peer, device_id_type=MESH)
    pl.semaphore_wait(barrier, len(peers))


def gather_kernel(nf, nc, comp_ref, info_ref, facs_ref, infos_ref, s1, r1, s2, r2, s3, r3, loc):
    f, c = lax.axis_index("fac"), lax.axis_index("cust")
    fp = [(lax.rem(f + d, nf), c) for d in range(1, nf)]
    half = nc // 2
    core = lax.rem(c, 2)
    twin = (f, c + 1 - 2 * core)
    sides = [lax.rem(c + 2 * d, nc) for d in range(1, half)]
    part = comp_ref.shape[0] // nc
    sync(fp + [(f, e) for e in sides] + [twin])

    def rows(q):
        return pl.ds(pl.multiple_of(q * part, part), part)

    def move(src, q, k, send, recv, peer, own=False):
        a = comp_ref.at[rows(q)] if own else facs_ref.at[src, rows(q)]
        b = info_ref.at[q] if own else infos_ref.at[src, q]
        pair = [
            pltpu.make_async_remote_copy(a, facs_ref.at[src, rows(q)], send.at[k, 0], recv.at[k, 0], device_id=peer, device_id_type=MESH),
            pltpu.make_async_remote_copy(b, infos_ref.at[src, q], send.at[k, 1], recv.at[k, 1], device_id=peer, device_id_type=MESH),
        ]
        for cpy in pair:
            cpy.start()
        return pair

    first = [move(f, c, d, s1, r1, peer, True) for d, peer in enumerate(fp)]
    own = pltpu.make_async_copy(comp_ref, facs_ref.at[f], loc.at[0])
    own.start()
    own_info = pltpu.make_async_copy(info_ref, infos_ref.at[f], loc.at[1])
    own_info.start()
    across, over = [], []
    for d in range(nf - 1):
        src = lax.rem(f + nf - 1 - d, nf)
        for cpy in first[d]:
            cpy.wait_recv()
        for e, q in enumerate(sides):
            across.append((src, lax.rem(c + nc - 2 * (e + 1), nc), move(src, c, d * (half - 1) + e, s2, r2, (f, q))))
        over.append(move(src, c, d * half, s3, r3, twin))
        for e in range(half - 1):
            if d > 0:
                ready = across[(d - 1) * (half - 1) + e]
                for cpy in ready[2]:
                    cpy.wait_recv()
                over.append(move(ready[0], ready[1], (d - 1) * half + 1 + e, s3, r3, twin))
    for e in range(half - 1):
        ready = across[(nf - 2) * (half - 1) + e]
        for cpy in ready[2]:
            cpy.wait_recv()
        over.append(move(ready[0], ready[1], (nf - 2) * half + 1 + e, s3, r3, twin))
    for pair in first + [a[2] for a in across]:
        for cpy in pair:
            cpy.wait_send()
    for pair in over:
        for cpy in pair:
            cpy.wait()
    own.wait()
    own_info.wait()


def step_kernel(step, facs_ref, infos_ref, mu_ref, load_ref, cust_t_ref, hq_ref, lam_ref, wt_ref, ext_ref,
                part_ref, mu_out_ref, lam_out_ref, tot_ref,
                info_ref, a_ref, w_ref, y_ref, x_ref, d_ref, acc_ref, cov_ref, soft_ref):
    first, size, prev = step == 0, 0.1 / (step + 1), 0.1 / max(step, 1)
    nf, n, width = facs_ref.shape
    cols = cust_t_ref.shape[1]
    block = y_ref.shape[2]
    tiles = cols // block
    lam = lam_ref[...]
    wt = wt_ref[...]
    a1, a2, a3 = split3(64.0 * lam - hq_ref[...])
    one_c = jnp.ones((3, cols), F32)
    mw = jnp.broadcast_to(-64.0 * wt, (3, cols))
    aug = jnp.concatenate([a1.astype(F32), a2.astype(F32), a3.astype(F32), one_c, mw, jnp.zeros((7, cols), F32)], axis=0)
    w_ref[0:width, :] = cust_t_ref[...]
    w_ref[width:width + 16, :] = aug.astype(BF16)
    w_ref[width + 16:, :] = jnp.zeros((width - 16, cols), BF16)
    cov_ref[...] = jnp.zeros_like(cov_ref)
    soft_ref[...] = jnp.zeros_like(soft_ref)
    lane = lax.broadcasted_iota(jnp.int32, (ROWS, width), 1)
    pad = jnp.where(lane == 3, -30000.0, 0.0).astype(BF16)
    sel = (lax.broadcasted_iota(jnp.int32, (16, width), 0) == lax.broadcasted_iota(jnp.int32, (16, width), 1)).astype(F32).astype(BF16)
    top = (lax.broadcasted_iota(jnp.int32, (16, 128), 0) == 0).astype(F32).astype(BF16)
    wrows = jnp.concatenate([wt, jnp.zeros((15, cols), F32)], axis=0).astype(BF16)
    d_ref[...] = lax.dot_general(wrows, top, (((0,), (0,)), ((), ())), preferred_element_type=F32).astype(BF16)
    nc, part = infos_ref.shape[1], infos_ref.shape[3]
    for f in range(nf):
        info_ref[f] = jnp.concatenate([infos_ref[f, p] for p in range(nc)], axis=1)
    offs = []
    off = jnp.int32(0)
    one_r = jnp.ones((3, n), F32)
    for f in range(nf):
        valid = info_ref[f, 0:1, :]
        cap = info_ref[f, 3:4, :]
        if first:
            mu = info_ref[f, 2:3, :]
        else:
            mu = mu_ref[f:f + 1, :]
            load = load_ref[f:f + 1, :]
            mu = jnp.maximum(0.0, mu + prev * (load - cap) / (load + jnp.where(valid > 0, cap, 1.0)))
        mu = mu * valid
        mu_out_ref[f:f + 1, :] = mu
        b = jnp.where(valid > 0, info_ref[f, 1:2, :], -30000.0)
        parts = [p.astype(F32) for p in split3(b) + split3(mu)]
        rows = jnp.concatenate([one_r] + parts + [jnp.zeros((7, n), F32)], axis=0).astype(BF16)
        side = lax.dot_general(rows, sel, (((0,), (0,)), ((), ())), preferred_element_type=F32).astype(BF16)
        count = jnp.sum(valid).astype(jnp.int32)
        off = pl.multiple_of(off, ALIGN)
        offs.append(off)
        a_ref[pl.ds(off, n), 0:width] = facs_ref[f]
        a_ref[pl.ds(off, n), width:2 * width] = side
        off = off + ((count + ALIGN - 1) // ALIGN) * ALIGN
    tail = pl.multiple_of(off, ALIGN)
    a_ref[pl.ds(tail, ROWS), 0:width] = jnp.zeros((ROWS, width), BF16)
    a_ref[pl.ds(tail, ROWS), width:2 * width] = pad
    n_blocks = (off + ROWS - 1) // ROWS
    scale = math.log2(math.e) / 6.4

    def body(i, _):
        base = pl.multiple_of(i * ROWS, ROWS)
        lhs = a_ref[pl.ds(base, ROWS), :]

        def dot(t):
            y_ref[t % 2] = jnp.dot(lhs, w_ref[:, t * block:(t + 1) * block], preferred_element_type=F32)

        dot(0)
        for t in range(tiles):
            if t + 1 < tiles:
                dot(t + 1)
            covs = [cov_ref[:, t * block + q * 128:t * block + (q + 1) * 128] for q in range(block // 128)]
            softs = [soft_ref[:, t * block + q * 128:t * block + (q + 1) * 128] for q in range(block // 128)]
            for r in range(0, ROWS, 32):
                for q in range(block // 128):
                    es = [jnp.exp2(y_ref[t % 2, r + 8 * s:r + 8 * s + 8, q * 128:(q + 1) * 128] * scale) for s in range(4)]
                    us = [1.0 + e for e in es]
                    p01 = us[0] * us[1]
                    p23 = us[2] * us[3]
                    r01 = 1.0 / p01
                    r23 = 1.0 / p23
                    xs = [es[0] * (us[1] * r01), es[1] * (us[0] * r01), es[2] * (us[3] * r23), es[3] * (us[2] * r23)]
                    covs[q] = covs[q] + ((xs[0] + xs[1]) + (xs[2] + xs[3]))
                    softs[q] = softs[q] + jnp.log(p01 * p23)
                    for h in range(2):
                        both = jnp.concatenate([xs[2 * h], xs[2 * h + 1]], axis=0).astype(BF16)
                        x_ref[t % 2, r + 16 * h:r + 16 * h + 16, q * 128:(q + 1) * 128] = both
            got = jnp.dot(x_ref[t % 2], d_ref[t * block:(t + 1) * block, :], preferred_element_type=F32)
            at = pl.ds(base, ROWS)
            acc_ref[at, :] = got if t == 0 else acc_ref[at, :] + got
            for q in range(block // 128):
                cov_ref[:, t * block + q * 128:t * block + (q + 1) * 128] = covs[q]
                soft_ref[:, t * block + q * 128:t * block + (q + 1) * 128] = softs[q]
        return 0

    lax.fori_loop(0, n_blocks, body, 0)
    diag = lax.broadcasted_iota(jnp.int32, (128, 128), 0) == lax.broadcasted_iota(jnp.int32, (128, 128), 1)
    for f in range(nf):
        for b in range(n // 128):
            at = pl.ds(pl.multiple_of(offs[f] + b * 128, ALIGN), 128)
            got = jnp.sum(jnp.where(diag, acc_ref[at, :], 0.0), axis=0, keepdims=True)
            part_ref[f:f + 1, b * 128:(b + 1) * 128] = jnp.where(info_ref[f, 0:1, b * 128:(b + 1) * 128] > 0, got, 0.0)
    cover = jnp.sum(cov_ref[...], axis=0, keepdims=True)
    soft = jnp.sum(soft_ref[...], axis=0, keepdims=True)
    me, c = lax.axis_index("fac"), lax.axis_index("cust")
    mine = jnp.sum(mu_out_ref[pl.ds(me, 1), :] * info_ref[me, 3:4, :])
    here = jnp.sum(wt * lam - TAU * wt * soft) - jnp.where(c == 0, mine, 0.0)
    spot = lax.broadcasted_iota(jnp.int32, (8, 128), 1) == step
    tot = ext_ref[...] + jnp.where(spot, here, 0.0)
    tot_ref[...] = tot
    if part_ref.shape[0] > nf:
        part_ref[nf:nf + 8, :] = jnp.zeros((8, n), F32)
        part_ref[nf:nf + 8, 0:128] = tot
    lam_out_ref[...] = lam + size * wt * (1.0 - cover) / (1.0 + cover)


def exchange(peers, src, slots, send, recv):
    copies = []
    for d, peer in enumerate(peers):
        cpy = pltpu.make_async_remote_copy(src, slots.at[d], send.at[d], recv.at[d], device_id=peer, device_id_type=MESH)
        cpy.start()
        copies.append(cpy)
    return copies


def reduce_kernel(nf, nc, x_ref, lam_ref, out_ref, lam_out, got1, mid, got2, s1, r1, s2, r2, s3, r3, loc):
    f, c = lax.axis_index("fac"), lax.axis_index("cust")
    fp = [(lax.rem(f + d, nf), c) for d in range(1, nf)]
    cp = [(f, lax.rem(c + d, nc)) for d in range(1, nc)]
    sync(fp + cp)
    first = exchange(cp, x_ref, got1, s1, r1)
    lams = []
    if lam_ref is not None:
        own = pltpu.make_async_copy(lam_ref, lam_out.at[f], loc)
        own.start()
        for d, peer in enumerate(fp):
            cpy = pltpu.make_async_remote_copy(lam_ref, lam_out.at[f], s3.at[d], r3.at[d], device_id=peer, device_id_type=MESH)
            cpy.start()
            lams.append(cpy)
    total = x_ref[...]
    for d, cpy in enumerate(first):
        cpy.wait()
        total = total + got1[d]
    mid[...] = total
    second = exchange(fp, mid, got2, s2, r2)
    for d, cpy in enumerate(second):
        cpy.wait()
        total = total + got2[d]
    out_ref[...] = total
    for cpy in lams:
        cpy.wait()
    if lam_ref is not None:
        own.wait()


def reduce_plain(nf, nc, x_ref, out_ref, got1, mid, got2, s1, r1, s2, r2):
    reduce_kernel(nf, nc, x_ref, None, out_ref, None, got1, mid, got2, s1, r1, s2, r2, None, None, None)


def finish_kernel(total_cust, total_ref, mu_ref, infos_ref, open_ref, shut_ref, out_ref, bound_ref):
    nf, nc = infos_ref.shape[0:2]
    n = open_ref.shape[1]
    f = lax.axis_index("fac")
    load = total_ref[pl.ds(f, 1), :]
    cap = jnp.concatenate([infos_ref[f, p, 3:4, :] for p in range(nc)], axis=1)
    new = jnp.maximum(0.0, mu_ref[pl.ds(f, 1), :] + (0.1 / ITERS) * (load - cap) / (load + jnp.where(cap > 0, cap, 1.0)))
    rows = jnp.concatenate([v.astype(F32) for v in split3(new)] + [jnp.zeros((13, n), F32)], axis=0).astype(BF16)
    got = jnp.dot(rows, onehot_of(open_ref[...]), preferred_element_type=F32)
    out_ref[...] = jnp.where(open_ref[...] > 0, got[0:1] + got[1:2] + got[2:3], shut_ref[...])
    bound_ref[...] = total_ref[nf:nf + 1, 0:128] / total_cust


def params(cid=None, mib=56):
    return pltpu.CompilerParams(collective_id=cid, has_side_effects=True, vmem_limit_bytes=mib * 2 ** 20) if cid is not None else pltpu.CompilerParams(vmem_limit_bytes=mib * 2 ** 20)


def local(nf, nc, fac_coords, cust_coords, open_flags, demand, fixed_cost, capacity, cap_mult, cover_mult):
    n, width = fac_coords.shape
    cols = cust_coords.shape[0]
    total_cust = cols * nf * nc
    sd = jax.ShapeDtypeStruct
    dma = pltpu.SemaphoreType.DMA
    part = n // nc
    open_row = open_flags.reshape(1, n)
    comp, info, cust_t, hq, wt, lam, ext, shut = pl.pallas_call(
        pre_kernel,
        out_shape=(sd((n, width), BF16), sd((nc, 8, part), F32), sd((width, cols), BF16), sd((1, cols), F32),
                   sd((1, cols), F32), sd((1, cols), F32), sd((8, 128), F32), sd((1, n), F32)),
        in_specs=[VMEM] * 8, out_specs=(VMEM,) * 8, compiler_params=params(), name="pre",
    )(open_row, fac_coords, capacity.reshape(1, n), cap_mult.reshape(1, n), fixed_cost.reshape(1, n), cust_coords,
      demand.reshape(1, nf * cols), cover_mult.reshape(1, nf * cols))
    sides = (nf - 1) * (nc // 2 - 1)
    facs, infos = pl.pallas_call(
        functools.partial(gather_kernel, nf, nc),
        out_shape=(sd((nf, n, width), BF16), sd((nf, nc, 8, part), F32)),
        in_specs=[VMEM] * 2, out_specs=(VMEM,) * 2,
        scratch_shapes=[dma((nf - 1, 2)), dma((nf - 1, 2)), dma((sides, 2)), dma((sides, 2)),
                        dma(((nf - 1) * (nc // 2), 2)), dma(((nf - 1) * (nc // 2), 2)), dma((2,))],
        compiler_params=params(0), name="gather",
    )(comp, info)
    block = math.gcd(cols, 512)
    total_rows = nf * n
    mu = load = hq
    tot = ext
    for step in range(ITERS):
        last = step == ITERS - 1
        rows = nf + 8 if last else nf
        payload, mu, lam, tot = pl.pallas_call(
            functools.partial(step_kernel, step),
            out_shape=(sd((rows, n), F32), sd((nf, n), F32), sd((1, cols), F32), sd((8, 128), F32)),
            in_specs=[VMEM] * 9, out_specs=(VMEM,) * 4,
            scratch_shapes=[
                pltpu.VMEM((nf, 8, n), F32),
                pltpu.VMEM((total_rows + n + ROWS, 2 * width), BF16),
                pltpu.VMEM((2 * width, cols), BF16),
                pltpu.VMEM((2, ROWS, block), F32),
                pltpu.VMEM((2, ROWS, block), BF16),
                pltpu.VMEM((cols, 128), BF16),
                pltpu.VMEM((total_rows + n + ROWS, 128), F32),
                pltpu.VMEM((8, cols), F32),
                pltpu.VMEM((8, cols), F32),
            ],
            compiler_params=params(), name="step",
        )(facs, infos, mu, load, cust_t, hq, lam, wt, tot)
        scratch = [pltpu.VMEM((nc - 1, rows, n), F32), pltpu.VMEM((rows, n), F32), pltpu.VMEM((nf - 1, rows, n), F32),
                   dma((nc - 1,)), dma((nc - 1,)), dma((nf - 1,)), dma((nf - 1,))]
        if not last:
            load = pl.pallas_call(
                functools.partial(reduce_plain, nf, nc),
                out_shape=sd((rows, n), F32), in_specs=[VMEM], out_specs=VMEM,
                scratch_shapes=scratch, compiler_params=params(1 + step), name="reduce",
            )(payload)
        else:
            load, lam_all = pl.pallas_call(
                functools.partial(reduce_kernel, nf, nc),
                out_shape=(sd((rows, n), F32), sd((nf, 1, cols), F32)), in_specs=[VMEM] * 2, out_specs=(VMEM,) * 2,
                scratch_shapes=scratch + [dma((nf - 1,)), dma((nf - 1,)), dma(())],
                compiler_params=params(1 + step), name="reduce",
            )(payload, lam)
    cap_final, bounds = pl.pallas_call(
        functools.partial(finish_kernel, total_cust), out_shape=(sd((1, n), F32), sd((1, 128), F32)),
        in_specs=[VMEM] * 5, out_specs=(VMEM,) * 2, compiler_params=params(), name="finish",
    )(load, mu, infos, open_row, shut)
    return lam_all.reshape(nf * cols), cap_final.reshape(n), bounds[0, :ITERS]


def solution(mesh):
    nf, nc = mesh.shape["fac"], mesh.shape["cust"]
    return jax.shard_map(
        functools.partial(local, nf, nc),
        mesh=mesh,
        in_specs=(P("fac", None), P(("cust", "fac"), None), P("fac"), P("cust"), P("fac"), P("fac"), P("fac"), P("cust")),
        out_specs=(P("cust"), P("fac"), P()),
        check_vma=False,
    )
```

time: 137 us -> 115 us (0.84)
  local copies, waits for them, and re-layouts: 9.55 us -> 1.8 us
  between operations: 6.38 us -> 0.68 us
  other arithmetic: 5.25 us -> 0 us
  Pallas kernels: 115 us -> 113 us
    pallas_call x9 -> x8, Pallas kernels: 92.3 us -> 86.5 us  [the longest x3 44.5 us: local(): pl.pallas_call(functools.partial(step_kernel, step), out_shape=(sd((rows,...]
    pallas_call x1, Pallas kernels: 22.5 us -> 26 us  [local(): pl.pallas_call(functools.partial(gather_kernel, nf, nc), out_shape=(sd((n...]
    slice x3 -> x0, local copies, waits for them, and re-layouts: 3.58 us -> none  [local(): tots.append(tot[0, 0])]
    dynamic_slice x2 -> x0, local copies, waits for them, and re-layouts: 2.62 us -> none  [the longest x1 1.33 us: local(): last = lax.dynamic_slice_in_dim(mu, f, 1, 0)]
    reduce_sum x2 -> x0, other arithmetic: 1.98 us -> none  [the longest x1 1.28 us: local(): fixed = jnp.sum(opened * fixed_cost - (1.0 - opened) * shut * capacity)]
where the time goes in v2:
time: 115 us
  Pallas kernels  113 us (98%)
  local copies, waits for them, and re-layouts  1.8 us (2%)
    pallas_call x3, Pallas kernels, local(): pl.pallas_call(functools.partial(step_kernel, step), out_shape=(sd((rows,...  44.5 us
    pallas_call x1, Pallas kernels, local(): pl.pallas_call(functools.partial(gather_kernel, nf, nc), out_shape=(sd((n...  26 us
    pallas_call x2, Pallas kernels, local(): pl.pallas_call(functools.partial(reduce_plain, nf, nc), out_shape=sd((row...  22.7 us
    pallas_call x1, Pallas kernels, local(): pl.pallas_call(functools.partial(reduce_kernel, nf, nc), out_shape=(sd((r...  14.5 us
    pallas_call x1, Pallas kernels, local(): pl.pallas_call(pre_kernel, out_shape=(sd((n, width), BF16), sd((nc, 8, pa...  2.76 us

profile of v2, /device:TPU:0, one launch (start us, length us, event | category | flops | bytes accessed | tf_op | source)
XLA Modules:
  0.0 115.0 jit_solution(260135992715028294)
XLA Ops:
  0.6 2.8 %pre.1 = (bf16[512,128]{1,0:T(8,128)(2,1)}, f32[4,8,128]{2,1,0:T(8,128)}, bf16[128,2048]{1,0:T(8,128)(2,1)}, f32[1,2048]{1,0:T(1,128)}, f32[1,2048]{1,0:T(1,128)...) custom-call(s32[1,512]{1,0:T(1,128)} %bitcast.13, bf16[512,128]{1,0:T(8,128)(2,1)} %fac_ref.1, ...), custom_call_target="tpu_custom_call" | custom-call | tf_op jit(solution)/shard_map/pre/pallas_call | solution.py:331
  3.4 26.0 %gather.1 = (bf16[8,512,128]{2,1,0:T(8,128)(2,1)}, f32[8,4,8,128]{3,2,1,0:T(8,128)}) custom-call(bf16[512,128]{1,0:T(8,128)(2,1)} %get-tuple-element.28.comp_ref, f32[4,8,128]{2,1,0:T(8,128)} %get-tuple-element.29.info_ref), custom_call_target="tpu_custom_call" | custom-call | tf_op jit(solution)/shard_map/gather/pallas_call | solution.py:339
  29.4 14.8 %step.3 = (f32[8,512]{1,0:T(8,128)}, f32[8,512]{1,0:T(8,128)}, f32[1,2048]{1,0:T(1,128)}, f32[8,128]{1,0:T(8,128)}) custom-call(bf16[8,512,128]{2,1,0:T(8,128)(2,1)} %get-tuple-element.30.facs_ref, f32[8,4,8,128]{3,2,1,0:T(8,128)} %get-tuple-element.31.infos_ref, f32[1,2048]{1,0:T(1,128)} %get-tuple-element.32.mu_ref.load_ref.hq_ref, ...), custom_call_target="tpu_custom_call" | custom-call | tf_op jit(solution)/shard_map/step/pallas_call | solution.py:354
  44.3 11.2 %reduce.3.load_ref = f32[8,512]{1,0:T(8,128)} custom-call(f32[8,512]{1,0:T(8,128)} %get-tuple-element.38.x_ref), custom_call_target="tpu_custom_call" | custom-call | tf_op jit(solution)/shard_map/reduce/pallas_call | solution.py:374
  55.4 14.8 %step.4 = (f32[8,512]{1,0:T(8,128)}, f32[8,512]{1,0:T(8,128)}, f32[1,2048]{1,0:T(1,128)}, f32[8,128]{1,0:T(8,128)}) custom-call(bf16[8,512,128]{2,1,0:T(8,128)(2,1)} %get-tuple-element.30.facs_ref, f32[8,4,8,128]{3,2,1,0:T(8,128)} %get-tuple-element.31.infos_ref, f32[8,512]{1,0:T(8,128)} %get-tuple-element.37.mu_ref, f32[8,512]{1,0:T(8,128)} %reduce.3.load_ref, ...), custom_call_target="tpu_custom_call" | custom-call | tf_op jit(solution)/shard_map/step/pallas_call | solution.py:354
  70.3 11.6 %reduce.4.load_ref = f32[8,512]{1,0:T(8,128)} custom-call(f32[8,512]{1,0:T(8,128)} %get-tuple-element.42.x_ref), custom_call_target="tpu_custom_call" | custom-call | tf_op jit(solution)/shard_map/reduce/pallas_call | solution.py:374
  81.9 14.9 %step.5 = (f32[16,512]{1,0:T(8,128)}, f32[8,512]{1,0:T(8,128)}, f32[1,2048]{1,0:T(1,128)}, f32[8,128]{1,0:T(8,128)}) custom-call(bf16[8,512,128]{2,1,0:T(8,128)(2,1)} %get-tuple-element.30.facs_ref, f32[8,4,8,128]{3,2,1,0:T(8,128)} %get-tuple-element.31.infos_ref, f32[8,512]{1,0:T(8,128)} %get-tuple-element.41.mu_ref, f32[8,512]{1,0:T(8,128)} %reduce.4.load_ref, ...), custom_call_target="tpu_custom_call" | custom-call | tf_op jit(solution)/shard_map/step/pallas_call | solution.py:354
  96.7 14.5 %reduce.5 = (f32[16,512]{1,0:T(8,128)}, f32[8,1,2048]{2,1,0:T(1,128)}) custom-call(f32[16,512]{1,0:T(8,128)} %get-tuple-element.45.x_ref, f32[1,2048]{1,0:T(1,128)} %get-tuple-element.46.lam_ref), custom_call_target="tpu_custom_call" | custom-call | tf_op jit(solution)/shard_map/reduce/pallas_call | solution.py:380
  111.3 0.0 copy-start
  111.3 2.0 %finish.1 = (f32[1,512]{1,0:T(1,128)}, f32[1,128]{1,0:T(1,128)}) custom-call(f32[16,512]{1,0:T(8,128)} %get-tuple-element.48.total_ref, f32[8,512]{1,0:T(8,128)} %get-tuple-element.49.mu_ref, f32[8,4,8,128]{3,2,1,0:T(8,128)} %get-tuple-element.31.infos_ref, s32[1,512]{1,0:T(1,128)} %bitcast.14, f32[1,512]{1,0:T(1,128)} %get-tuple-element.50.shut_ref), custom_call_target="tpu_custom_call" | custom-call | tf_op jit(solution)/shard_map/finish/pallas_call | solution.py:386
  113.2 0.0 copy-start.1
  113.2 0.7 copy-done.1
  113.9 0.5 slice_bitcast_fusion
  114.4 0.0 copy-done
  114.4 0.6 copy.12
Async XLA Ops:
  111.3 3.1 %copy-start = (f32[8,1,2048]{2,1,0:T(1,128)S(1)}, f32[8,1,2048]{2,1,0:T(1,128)}, u32[]{:S(2)}) copy-start(f32[8,1,2048]{2,1,0:T(1,128)} %get-tuple-element.47) | copy-start | bytes 196612
  113.2 0.7 copy-start.1
